TPU v7x, 32 devices: a whole 2x2x4 slice. The times are simulated.
32 devices in a mesh: beta: 16 (over z, y, x), grp: 2 (over core).
Axes of the slice: x: 2, y: 2, z: 4, core: 2. Of those that a mesh axis runs over, the one named last changes fastest.
Arguments:
- samples: float32 [128, 8, 128, 128], P('beta', 'grp'), parts along dimension 1, may hold values from -6 to 6
Outputs:
- coeffs: float32 [128, 2, 8, 64, 64], P('beta', None, 'grp'), parts along dimension 2
- power: float32 [8, 64], P('grp'), parts along dimension 0
There are 2 independent parts, one for each index of `grp`. A program takes and returns all parts, laid end to end along the dimension named above; each array names one. Nothing has to cross between parts.
All inputs are finite; a program needn't handle non-finite values.
Results may differ from a plain program's by a relative error of at most 0.0003.
Values sent between devices are 32-bit elements; how exact they have to be, the bound alone decides.
No kernel may reach another device: no remote copies, remote signals or barrier semaphores. Data moves between devices by JAX's collectives and lax.ppermute only.
A program may use at most 64 MiB of HBM per device.

v0:
```python
import jax
import jax.numpy as jnp
from jax import lax
from jax.sharding import PartitionSpec as P

HIGHEST = lax.Precision.HIGHEST


def beta_angles(spread):
    grid_size = 2 * spread
    return (2.0 * jnp.arange(grid_size, dtype=jnp.float32) + 1.0) * (jnp.pi / (4.0 * spread))


def quadrature(spread):
    angles = beta_angles(spread)
    odd_terms = 2.0 * jnp.arange(spread, dtype=jnp.float32) + 1.0
    series = jnp.sum(jnp.sin(angles[:, None] * odd_terms[None, :]) / odd_terms[None, :], axis=1)
    return 2.0 / spread * jnp.sin(angles) * series


def gamma_table(spread):
    grid_size = 2 * spread
    positions = jnp.arange(grid_size, dtype=jnp.int32)
    orders = jnp.arange(spread, dtype=jnp.int32)
    phase_index = positions[:, None] * orders[None, :] % grid_size
    angles = phase_index.astype(jnp.float32) * (2.0 * jnp.pi / grid_size)
    return jnp.concatenate([jnp.cos(angles), -jnp.sin(angles)], axis=1)


def alpha_table(spread, row_index):
    grid_size = 2 * spread
    positions = jnp.arange(grid_size, dtype=jnp.int32)
    phase_index = row_index[:, None] * positions[None, :] % grid_size
    angles = phase_index.astype(jnp.float32) * (2.0 * jnp.pi / grid_size)
    cosine = jnp.cos(angles) / grid_size
    sine_part = jnp.sin(angles) / grid_size
    real_rows = jnp.stack([cosine, sine_part], axis=1)
    imag_rows = jnp.stack([-sine_part, cosine], axis=1)
    return jnp.stack([real_rows, imag_rows], axis=0)


def log_factorial(value, float_type):
    return lax.lgamma((value + 1).astype(float_type))


def wigner_start(alpha_order, gamma_order, log_cosine, log_sine):
    float_type = log_cosine.dtype
    lowest = jnp.maximum(jnp.abs(alpha_order), gamma_order)
    shift_low = jnp.maximum(0, gamma_order - alpha_order)
    magnitude = 0.5 * (
        log_factorial(lowest + alpha_order, float_type)
        + log_factorial(lowest - alpha_order, float_type)
        + log_factorial(lowest + gamma_order, float_type)
        + log_factorial(lowest - gamma_order, float_type)
    )
    magnitude = (
        magnitude
        - log_factorial(lowest + gamma_order - shift_low, float_type)
        - log_factorial(shift_low, float_type)
    )
    magnitude = magnitude - log_factorial(alpha_order - gamma_order + shift_low, float_type)
    magnitude = magnitude - log_factorial(lowest - alpha_order - shift_low, float_type)
    cos_power = (2 * lowest + gamma_order - alpha_order - 2 * shift_low).astype(float_type)
    sin_power = (alpha_order - gamma_order + 2 * shift_low).astype(float_type)
    parity = (alpha_order - gamma_order + shift_low) % 2
    sign_factor = (1 - 2 * parity).astype(float_type)
    return sign_factor * jnp.exp(magnitude + cos_power * log_cosine + sin_power * log_sine)


def advance(degree, carried, alpha_order, gamma_order, cos_angles, start_value, lowest):
    former, current = carried
    float_type = current.dtype
    previous = (degree - 1).astype(float_type)
    alpha_float = alpha_order.astype(float_type)
    gamma_float = gamma_order.astype(float_type)
    cross_ratio = alpha_float * gamma_float / jnp.maximum(previous * (previous + 1.0), 1.0)
    upper_term = ((previous + 1.0) * (previous + 1.0) - alpha_float * alpha_float) * (
        (previous + 1.0) * (previous + 1.0) - gamma_float * gamma_float
    )
    lower_term = (previous * previous - alpha_float * alpha_float) * (
        previous * previous - gamma_float * gamma_float
    )
    root_upper = jnp.sqrt(jnp.maximum(upper_term, 1.0))
    forward = (previous + 1.0) * (2.0 * previous + 1.0) / root_upper
    backward = (
        (previous + 1.0)
        * jnp.sqrt(jnp.maximum(lower_term, 0.0))
        / (jnp.maximum(previous, 1.0) * root_upper)
    )
    recurred = forward * (cos_angles - cross_ratio) * current - backward * former
    renewed = jnp.where(degree == lowest, start_value, recurred)
    return (current, renewed)


def degree_rows(row_index, weighted, spread):
    stride = 8
    grid_size = 2 * spread
    group_size = row_index.shape[0]
    channels = weighted.shape[2]
    block_count = spread // stride
    alpha_order = jnp.where(row_index < spread, row_index, row_index - grid_size)[:, None, None]
    gamma_order = jnp.arange(spread, dtype=jnp.int32)[None, None, :]
    angles = beta_angles(spread)
    cos_angles = jnp.cos(angles)[None, :, None]
    log_cosine = jnp.log(jnp.cos(0.5 * angles))[None, :, None]
    log_sine = jnp.log(jnp.sin(0.5 * angles))[None, :, None]
    lowest = jnp.maximum(jnp.abs(alpha_order), gamma_order)
    start_value = wigner_start(alpha_order, gamma_order, log_cosine, log_sine)
    first_block = jnp.min(jnp.abs(alpha_order)) // stride
    empty_state = jnp.zeros((group_size, grid_size, spread), jnp.float32)

    def compute_block(operands):
        block_index, former, current = operands
        levels = []
        for offset in range(stride):
            former, current = advance(
                block_index * stride + offset,
                (former, current),
                alpha_order,
                gamma_order,
                cos_angles,
                start_value,
                lowest,
            )
            levels.append(current)
        stacked = jnp.stack(levels, axis=0)
        block_part = jnp.einsum("jgkq,kgcq->gcjq", stacked, weighted, precision=HIGHEST)
        return (former, current, block_part)

    def skip_block(operands):
        block_index, former, current = operands
        return (former, current, jnp.zeros((group_size, channels, stride, spread), jnp.float32))

    def block_step(carried, block_index):
        former, current = carried
        former, current, block_part = lax.cond(
            block_index >= first_block, compute_block, skip_block, (block_index, former, current)
        )
        return ((former, current), block_part)

    _, parts = lax.scan(
        block_step, (empty_state, empty_state), jnp.arange(block_count, dtype=jnp.int32)
    )
    output = jnp.transpose(parts, (1, 2, 0, 3, 4)).reshape(group_size, channels, spread, spread)
    degree_scale = 8.0 * jnp.sqrt(2.0 * jnp.arange(spread, dtype=jnp.float32) + 1.0)
    return output * degree_scale[None, None, :, None]


def degree_energy(coeffs, functions, spread):
    split_view = coeffs.reshape(coeffs.shape[0], 2, functions, spread, spread)
    multiplicity = jnp.where(jnp.arange(spread) == 0, 1.0, 2.0).astype(jnp.float32)
    energy_sum = jnp.sum(split_view * split_view * multiplicity, axis=(0, 1, 4))
    degrees = 2.0 * jnp.arange(spread, dtype=jnp.float32) + 1.0
    return energy_sum / (degrees * degrees)[None, :]


def local(samples):
    devices = lax.axis_size("beta")
    device = lax.axis_index("beta")
    local_beta = samples.shape[0]
    functions = samples.shape[1]
    grid_size = samples.shape[2]
    spread = grid_size // 2
    channels = 2 * functions
    row_count = grid_size // devices
    natural_rows = jnp.arange(grid_size, dtype=jnp.int32)
    halfway = jnp.einsum("kfag,gx->kfax", samples, gamma_table(spread), precision=HIGHEST)
    halfway = halfway.reshape(local_beta, functions, grid_size, 2, spread)
    spectrum = jnp.einsum(
        "kfacq,spca->kpsfq", halfway, alpha_table(spread, natural_rows), precision=HIGHEST
    )
    spectrum = spectrum.reshape(local_beta, grid_size, channels, spread)
    received = lax.all_to_all(spectrum, "beta", split_axis=1, concat_axis=0, tiled=True)
    weighted = received * quadrature(spread)[:, None, None, None]
    owned_rows = lax.dynamic_slice_in_dim(natural_rows, device * row_count, row_count)
    computed = degree_rows(owned_rows, weighted, spread)
    power_part = degree_energy(computed, functions, spread)
    coeffs = computed
    power = lax.psum(power_part, "beta")
    coeffs = coeffs.reshape(row_count, 2, functions, spread, spread)
    return (coeffs, power)


def solution(mesh):
    return jax.shard_map(
        local,
        mesh=mesh,
        in_specs=(P("beta", "grp", None, None),),
        out_specs=(P("beta", None, "grp", None, None), P("grp", None)),
        check_vma=False,
    )
```

profile of v0, /device:TPU:0, one launch (start us, length us, event | category | flops | bytes accessed | tf_op | source)
XLA Modules:
  0.0 345.6 jit_solution(5608972519271680303)
XLA Ops:
  18.8 8.4 %all-to-all-start = ((f32[16,1,32768]{2,1,0:T(1,128)}), f32[16,1,32768]{2,1,0:T(1,128)}, u32[]{:S(2)}, u32[]{:S(2)}) async-start(f32[16,1,32768]{2,1,0:T(1,128)} %reshape.2457), calls=%async_computation | async-start | bytes 4194304 | tf_op jit(solution)/shard_map/all_to_all | solution.py:173
  32.1 38.1 %all-to-all-done = f32[16,1,32768]{2,1,0:T(1,128)} async-done(((f32[16,1,32768]{2,1,0:T(1,128)}), f32[16,1,32768]{2,1,0:T(1,128)}, u32[]{:S(2)}, u32[]{:S(2)}) %all-to-all-start) | async-done | bytes 2097184 | tf_op jit(solution)/shard_map/all_to_all | solution.py:173
  70.9 8.6 %reduce.3 = f32[16,32768]{1,0:T(8,128)} reduce(f32[16,1,32768]{2,1,0:T(1,128)} %all-to-all-done, f32[]{:T(128)} %broadcast.2681), dimensions={1}, to_apply=%all_to_all.13.reduce_sub_computation | reduce | bytes 4194308 | tf_op jit(solution)/shard_map/all_to_all | solution.py:173
  93.9 182.8 %while.16 = (s32[]{:T(128)}, f32[8,128,64]{1,2,0:T(8,128)S(1)}, f32[8,128,64]{1,2,0:T(8,128)S(1)}, f32[8,8,8,8,64]{2,3,4,1,0:T(8,128)}, s32[8]{0:T(128)S(1)}, /*...) while((s32[]{:T(128)}, f32[8,128,64]{1,2,0:T(8,128)S(1)}, ...), condition=%wide.region_5.6_spmd.clone.clone, body=%wide.region_2.5_spmd.clone.clone.sunk | while | flops 53850804 | bytes 15474387 | solution.py:141
  95.2 18.6 %conditional.4 = (f32[8,128,64]{1,2,0:T(8,128)S(1)}, f32[8,128,64]{1,2,0:T(8,128)S(1)}, f32[1,8,8,8,64]{2,3,4,1,0:T(8,128)}) conditional(s32[]{:T(128)} %convert_element_type.412, (f32[8,128,64]{1,2,0:T(8,128)S(1)}, f32[8,128,64]{1,2,0:T(8,128)S(1)}) %tuple.139, (s32[]{:T(128)}, s32[8]{0:T(128)S(1)}, s32[8,1,1]{0,2,1:T(1,128)S(1)}, ...), branch_computations={%region_3.3_spmd, %region_4.4_spmd.clone} | conditional | flops 53850800 | bytes 11276004 | solution.py:136
  100.7 6.2 %stack.51 = f32[8,8,128,64]{2,0,3,1:T(8,128)} concatenate(f32[1,8,128,64]{2,0,3,1:T(1,128)} %bitcast.229, f32[1,8,128,64]{2,0,3,1:T(1,128)} %bitcast.228, f32[1,8,128,64]{2,0,3,1:T(1,128)} %bitcast.227, f32[1,8,128,64]{2,0,3,1:T(1,128)S(1)} %bitcast.226, f32[1,8,128,64]{2,0,3,1:T(1,128)S(1)} %bitcast.225, f32[1,8,128,64]{2,0,3,1:T(1,128)S(1)} %bitcast.224, ...), dimensions={0} | concatenate | bytes 4194304 | tf_op jit(solution)/shard_map/while/body/eval_jaxpr/cond/branch_1_fun/stack | solution.py:126
  106.9 6.9 %convolution_bitcast_fusion = f32[1,8,8,8,64]{2,3,4,1,0:T(8,128)} fusion(f32[8,8,128,64]{2,0,3,1:T(8,128)} %stack.51, f32[128,8,8,64]{0,2,3,1:T(8,128)} %get-tuple-element.428), kind=kOutput, calls=%fused_computation.4 | convolution fusion | flops 50331648 | bytes 4325376 | tf_op jit(solution)/shard_map/while/body/eval_jaxpr/cond/branch_1_fun/jgkq,kgcq->gcjq/dot_general | solution.py:127
  118.1 18.6 %conditional.4 = (f32[8,128,64]{1,2,0:T(8,128)S(1)}, f32[8,128,64]{1,2,0:T(8,128)S(1)}, f32[1,8,8,8,64]{2,3,4,1,0:T(8,128)}) conditional(s32[]{:T(128)} %convert_element_type.412, (f32[8,128,64]{1,2,0:T(8,128)S(1)}, f32[8,128,64]{1,2,0:T(8,128)S(1)}) %tuple.139, (s32[]{:T(128)}, s32[8]{0:T(128)S(1)}, s32[8,1,1]{0,2,1:T(1,128)S(1)}, ...), branch_computations={%region_3.3_spmd, %region_4.4_spmd.clone} | conditional | flops 53850800 | bytes 11276004 | solution.py:136
  129.7 6.9 %convolution_bitcast_fusion = f32[1,8,8,8,64]{2,3,4,1,0:T(8,128)} fusion(f32[8,8,128,64]{2,0,3,1:T(8,128)} %stack.51, f32[128,8,8,64]{0,2,3,1:T(8,128)} %get-tuple-element.428), kind=kOutput, calls=%fused_computation.4 | convolution fusion | flops 50331648 | bytes 4325376 | tf_op jit(solution)/shard_map/while/body/eval_jaxpr/cond/branch_1_fun/jgkq,kgcq->gcjq/dot_general | solution.py:127
  140.9 18.6 %conditional.4 = (f32[8,128,64]{1,2,0:T(8,128)S(1)}, f32[8,128,64]{1,2,0:T(8,128)S(1)}, f32[1,8,8,8,64]{2,3,4,1,0:T(8,128)}) conditional(s32[]{:T(128)} %convert_element_type.412, (f32[8,128,64]{1,2,0:T(8,128)S(1)}, f32[8,128,64]{1,2,0:T(8,128)S(1)}) %tuple.139, (s32[]{:T(128)}, s32[8]{0:T(128)S(1)}, s32[8,1,1]{0,2,1:T(1,128)S(1)}, ...), branch_computations={%region_3.3_spmd, %region_4.4_spmd.clone} | conditional | flops 53850800 | bytes 11276004 | solution.py:136
  152.5 6.9 %convolution_bitcast_fusion = f32[1,8,8,8,64]{2,3,4,1,0:T(8,128)} fusion(f32[8,8,128,64]{2,0,3,1:T(8,128)} %stack.51, f32[128,8,8,64]{0,2,3,1:T(8,128)} %get-tuple-element.428), kind=kOutput, calls=%fused_computation.4 | convolution fusion | flops 50331648 | bytes 4325376 | tf_op jit(solution)/shard_map/while/body/eval_jaxpr/cond/branch_1_fun/jgkq,kgcq->gcjq/dot_general | solution.py:127
  163.7 18.6 %conditional.4 = (f32[8,128,64]{1,2,0:T(8,128)S(1)}, f32[8,128,64]{1,2,0:T(8,128)S(1)}, f32[1,8,8,8,64]{2,3,4,1,0:T(8,128)}) conditional(s32[]{:T(128)} %convert_element_type.412, (f32[8,128,64]{1,2,0:T(8,128)S(1)}, f32[8,128,64]{1,2,0:T(8,128)S(1)}) %tuple.139, (s32[]{:T(128)}, s32[8]{0:T(128)S(1)}, s32[8,1,1]{0,2,1:T(1,128)S(1)}, ...), branch_computations={%region_3.3_spmd, %region_4.4_spmd.clone} | conditional | flops 53850800 | bytes 11276004 | solution.py:136
  175.3 6.9 %convolution_bitcast_fusion = f32[1,8,8,8,64]{2,3,4,1,0:T(8,128)} fusion(f32[8,8,128,64]{2,0,3,1:T(8,128)} %stack.51, f32[128,8,8,64]{0,2,3,1:T(8,128)} %get-tuple-element.428), kind=kOutput, calls=%fused_computation.4 | convolution fusion | flops 50331648 | bytes 4325376 | tf_op jit(solution)/shard_map/while/body/eval_jaxpr/cond/branch_1_fun/jgkq,kgcq->gcjq/dot_general | solution.py:127
  186.5 18.6 %conditional.4 = (f32[8,128,64]{1,2,0:T(8,128)S(1)}, f32[8,128,64]{1,2,0:T(8,128)S(1)}, f32[1,8,8,8,64]{2,3,4,1,0:T(8,128)}) conditional(s32[]{:T(128)} %convert_element_type.412, (f32[8,128,64]{1,2,0:T(8,128)S(1)}, f32[8,128,64]{1,2,0:T(8,128)S(1)}) %tuple.139, (s32[]{:T(128)}, s32[8]{0:T(128)S(1)}, s32[8,1,1]{0,2,1:T(1,128)S(1)}, ...), branch_computations={%region_3.3_spmd, %region_4.4_spmd.clone} | conditional | flops 53850800 | bytes 11276004 | solution.py:136
  198.2 6.9 %convolution_bitcast_fusion = f32[1,8,8,8,64]{2,3,4,1,0:T(8,128)} fusion(f32[8,8,128,64]{2,0,3,1:T(8,128)} %stack.51, f32[128,8,8,64]{0,2,3,1:T(8,128)} %get-tuple-element.428), kind=kOutput, calls=%fused_computation.4 | convolution fusion | flops 50331648 | bytes 4325376 | tf_op jit(solution)/shard_map/while/body/eval_jaxpr/cond/branch_1_fun/jgkq,kgcq->gcjq/dot_general | solution.py:127
  209.4 18.6 %conditional.4 = (f32[8,128,64]{1,2,0:T(8,128)S(1)}, f32[8,128,64]{1,2,0:T(8,128)S(1)}, f32[1,8,8,8,64]{2,3,4,1,0:T(8,128)}) conditional(s32[]{:T(128)} %convert_element_type.412, (f32[8,128,64]{1,2,0:T(8,128)S(1)}, f32[8,128,64]{1,2,0:T(8,128)S(1)}) %tuple.139, (s32[]{:T(128)}, s32[8]{0:T(128)S(1)}, s32[8,1,1]{0,2,1:T(1,128)S(1)}, ...), branch_computations={%region_3.3_spmd, %region_4.4_spmd.clone} | conditional | flops 53850800 | bytes 11276004 | solution.py:136
  221.0 6.9 %convolution_bitcast_fusion = f32[1,8,8,8,64]{2,3,4,1,0:T(8,128)} fusion(f32[8,8,128,64]{2,0,3,1:T(8,128)} %stack.51, f32[128,8,8,64]{0,2,3,1:T(8,128)} %get-tuple-element.428), kind=kOutput, calls=%fused_computation.4 | convolution fusion | flops 50331648 | bytes 4325376 | tf_op jit(solution)/shard_map/while/body/eval_jaxpr/cond/branch_1_fun/jgkq,kgcq->gcjq/dot_general | solution.py:127
  232.2 18.6 %conditional.4 = (f32[8,128,64]{1,2,0:T(8,128)S(1)}, f32[8,128,64]{1,2,0:T(8,128)S(1)}, f32[1,8,8,8,64]{2,3,4,1,0:T(8,128)}) conditional(s32[]{:T(128)} %convert_element_type.412, (f32[8,128,64]{1,2,0:T(8,128)S(1)}, f32[8,128,64]{1,2,0:T(8,128)S(1)}) %tuple.139, (s32[]{:T(128)}, s32[8]{0:T(128)S(1)}, s32[8,1,1]{0,2,1:T(1,128)S(1)}, ...), branch_computations={%region_3.3_spmd, %region_4.4_spmd.clone} | conditional | flops 53850800 | bytes 11276004 | solution.py:136
  243.8 6.9 %convolution_bitcast_fusion = f32[1,8,8,8,64]{2,3,4,1,0:T(8,128)} fusion(f32[8,8,128,64]{2,0,3,1:T(8,128)} %stack.51, f32[128,8,8,64]{0,2,3,1:T(8,128)} %get-tuple-element.428), kind=kOutput, calls=%fused_computation.4 | convolution fusion | flops 50331648 | bytes 4325376 | tf_op jit(solution)/shard_map/while/body/eval_jaxpr/cond/branch_1_fun/jgkq,kgcq->gcjq/dot_general | solution.py:127
  255.0 18.6 %conditional.4 = (f32[8,128,64]{1,2,0:T(8,128)S(1)}, f32[8,128,64]{1,2,0:T(8,128)S(1)}, f32[1,8,8,8,64]{2,3,4,1,0:T(8,128)}) conditional(s32[]{:T(128)} %convert_element_type.412, (f32[8,128,64]{1,2,0:T(8,128)S(1)}, f32[8,128,64]{1,2,0:T(8,128)S(1)}) %tuple.139, (s32[]{:T(128)}, s32[8]{0:T(128)S(1)}, s32[8,1,1]{0,2,1:T(1,128)S(1)}, ...), branch_computations={%region_3.3_spmd, %region_4.4_spmd.clone} | conditional | flops 53850800 | bytes 11276004 | solution.py:136
  266.7 6.9 %convolution_bitcast_fusion = f32[1,8,8,8,64]{2,3,4,1,0:T(8,128)} fusion(f32[8,8,128,64]{2,0,3,1:T(8,128)} %stack.51, f32[128,8,8,64]{0,2,3,1:T(8,128)} %get-tuple-element.428), kind=kOutput, calls=%fused_computation.4 | convolution fusion | flops 50331648 | bytes 4325376 | tf_op jit(solution)/shard_map/while/body/eval_jaxpr/cond/branch_1_fun/jgkq,kgcq->gcjq/dot_general | solution.py:127
  276.7 11.1 %copy.62 = f32[8,8,8,8,64]{4,3,2,1,0:T(8,128)} copy(f32[8,8,8,8,64]{1,3,4,0,2:T(8,128)} %bitcast.221) | data formatting | bytes 2097152 | tf_op jit(solution)/shard_map/transpose | solution.py:144
  287.8 8.5 %multiply_reduce_fusion = f32[8,8,8]{0,2,1:T(8,128)S(1)} fusion(f32[64]{0:T(128)S(1)} %compare_select_fusion.9, f32[8,8]{1,0:T(8,128)S(1)} %sqrt_multiply_fusion, f32[8,8,8,8,64]{2,3,4,1,0:T(8,128)} %get-tuple-element.216), kind=kLoop, calls=%fused_computation.97 | loop fusion | flops 1048064 | bytes 1051136 | tf_op jit(solution)/shard_map/reduce_sum | solution.py:152
  296.5 45.8 %psum.7 = f32[4,64]{1,0:T(4,128)} all-reduce(f32[4,64]{1,0:T(4,128)S(1)} %broadcast_divide_fusion), channel_id=1, replica_groups=mesh['beta'=16,'grp'=2] {'beta'}, use_global_device_ids=true, to_apply=%region_8.9 | all-reduce | flops 256 | bytes 2048 | tf_op jit(solution)/shard_map/psum | solution.py:179
  (304 shorter events, 148.0 us)
Async XLA Ops:
  0.6 1.6 copy-start
  18.8 51.5 %all-to-all-start = ((f32[16,1,32768]{2,1,0:T(1,128)}), f32[16,1,32768]{2,1,0:T(1,128)}, u32[]{:S(2)}, u32[]{:S(2)}) async-start(f32[16,1,32768]{2,1,0:T(1,128)} %reshape.2457), calls=%async_computation | async-start | bytes 4194304 | tf_op jit(solution)/shard_map/all_to_all | solution.py:173
  94.1 1.1 copy-start.2
  113.8 3.1 copy-start.3
  116.9 1.1 copy-start.2
  136.7 3.1 copy-start.3
  139.7 1.1 copy-start.2
  159.5 3.1 copy-start.3
  162.6 1.1 copy-start.2
  182.3 3.1 copy-start.3
  185.4 1.1 copy-start.2
  205.1 3.1 copy-start.3
  208.3 1.1 copy-start.2
  228.0 3.1 copy-start.3
  231.1 1.1 copy-start.2
  250.8 3.1 copy-start.3
  253.9 1.1 copy-start.2
  273.6 3.0 copy-start.3
  287.8 8.7 %copy-start.1 = (f32[64]{0:T(128)S(1)}, f32[64]{0:T(128)}, u32[]{:S(2)}) copy-start(f32[64]{0:T(128)} %fusion.87) | copy-start | bytes 772
where the time goes:
time: 351 us; the launch traced here: 346 us
  local copies, waits for them, and re-layouts  117 us (33%)
  other arithmetic  62.1 us (18%)
  matrix products  59.5 us (17%)
  blocking collectives  45.8 us (13%)
  waiting for transfers between devices  38.1 us (11%)
  loops' own time  11.6 us (3%)
  starting transfers between devices  8.4 us (2%)
  between operations  3.57 us (1%)
    dot_general x8, matrix products, compute_block(): jnp.einsum('jgkq,kgcq->gcjq', stacked, weighted, precision=HIGHEST)  55.6 us
    another operation x8, local copies, waits for them, and re-layouts, compute_block(): stacked = jnp.stack(levels, axis=0)  49.9 us
    psum x1, blocking collectives, local(): power = lax.psum(power_part, 'beta')  45.8 us
    all_to_all x1, waiting for transfers between devices, local(): lax.all_to_all(spectrum, 'beta', split_axis=1, concat_axis=0, tiled=True)  38.1 us
    select_n x8, other arithmetic, advance(): renewed = jnp.where(degree == lowest, start_value, recurred)  28.7 us
    dynamic_update_slice x8, local copies, waits for them, and re-layouts, degree_rows(): lax.scan(block_step, (empty_state, empty_state), jnp.arange(block_count,...  24.7 us
    unnamed x7, local copies, waits for them, and re-layouts  15.6 us
    transpose x1, local copies, waits for them, and re-layouts, degree_rows(): jnp.transpose(parts, (1, 2, 0, 3, 4))  11.1 us
  transfers between devices with their start and end apart: 1, of which 1 were waited for; matrix products, arithmetic and copies ran while one was open for 1% of the time, Pallas kernels for 0%

commit v1 on v0

--- a/solution.py
+++ b/solution.py
@@ -176,7 +176,10 @@
     computed = degree_rows(owned_rows, weighted, spread)
     power_part = degree_energy(computed, functions, spread)
     coeffs = computed
-    power = lax.psum(power_part, "beta")
+    devices_2, power = (lax.axis_size("beta"), power_part)
+    for far in [1 << k for k in range(devices_2.bit_length() - 1)]:
+        pairs = [(i, i ^ far) for i in range(devices_2)]
+        power = power + lax.ppermute(power, "beta", pairs)
     coeffs = coeffs.reshape(row_count, 2, functions, spread, spread)
     return (coeffs, power)
 

time: 351 us -> 321 us (0.915)
  blocking collectives: 45.8 us -> 0 us
  waiting for transfers between devices: 38.1 us -> 46.2 us
  starting transfers between devices: 8.4 us -> 14.8 us
    psum x1 -> x0, blocking collectives: 45.8 us -> none  [local(): power = lax.psum(power_part, 'beta')]
    ppermute x0 -> x4, waiting for transfers between devices: none -> 7.16 us  [local(): power = power + lax.ppermute(power, 'beta', pairs)]
    ppermute x0 -> x4, starting transfers between devices: none -> 6.41 us  [local(): power = power + lax.ppermute(power, 'beta', pairs)]
    unnamed x7 -> x5, local copies, waits for them, and re-layouts: 15.6 us -> 15.6 us
  transfers between devices with their start and end apart: 1 -> 5, of which waited for: 1 -> 3; matrix products, arithmetic and copies ran while one was open for 1% -> 5% of each run, Pallas kernels for 0% -> 0%
where the time goes in v1:
time: 321 us; the launch traced here: 315 us
  local copies, waits for them, and re-layouts  117 us (36%)
  other arithmetic  61.8 us (19%)
  matrix products  59.4 us (19%)
  waiting for transfers between devices  46.2 us (14%)
  starting transfers between devices  14.8 us (5%)
  loops' own time  12.9 us (4%)
  between operations  3.31 us (1%)
    dot_general x8, matrix products, compute_block(): jnp.einsum('jgkq,kgcq->gcjq', stacked, weighted, precision=HIGHEST)  55.5 us
    another operation x8, local copies, waits for them, and re-layouts, compute_block(): stacked = jnp.stack(levels, axis=0)  50 us
    all_to_all x1, waiting for transfers between devices, local(): lax.all_to_all(spectrum, 'beta', split_axis=1, concat_axis=0, tiled=True)  39 us
    select_n x8, other arithmetic, advance(): renewed = jnp.where(degree == lowest, start_value, recurred)  28.4 us
    dynamic_update_slice x8, local copies, waits for them, and re-layouts, degree_rows(): lax.scan(block_step, (empty_state, empty_state), jnp.arange(block_count,...  24.7 us
    unnamed x5, local copies, waits for them, and re-layouts  15.6 us
    transpose x1, local copies, waits for them, and re-layouts, degree_rows(): jnp.transpose(parts, (1, 2, 0, 3, 4))  11.1 us
    all_to_all x1, other arithmetic, local(): lax.all_to_all(spectrum, 'beta', split_axis=1, concat_axis=0, tiled=True)  8.58 us
  transfers between devices with their start and end apart: 5, of which 3 were waited for; matrix products, arithmetic and copies ran while one was open for 5% of the time, Pallas kernels for 0%

profile of v1, /device:TPU:0, one launch (start us, length us, event | category | flops | bytes accessed | tf_op | source)
XLA Modules:
  0.0 315.3 jit_solution(262321723986800368)
XLA Ops:
  18.8 8.4 %all-to-all-start = ((f32[16,1,32768]{2,1,0:T(1,128)}), f32[16,1,32768]{2,1,0:T(1,128)}, u32[]{:S(2)}, u32[]{:S(2)}) async-start(f32[16,1,32768]{2,1,0:T(1,128)} %reshape.2457), calls=%async_computation | async-start | bytes 4194304 | tf_op jit(solution)/shard_map/all_to_all | solution.py:173
  31.3 39.0 %all-to-all-done = f32[16,1,32768]{2,1,0:T(1,128)} async-done(((f32[16,1,32768]{2,1,0:T(1,128)}), f32[16,1,32768]{2,1,0:T(1,128)}, u32[]{:S(2)}, u32[]{:S(2)}) %all-to-all-start) | async-done | bytes 2097184 | tf_op jit(solution)/shard_map/all_to_all | solution.py:173
  70.8 8.6 %reduce.3 = f32[16,32768]{1,0:T(8,128)} reduce(f32[16,1,32768]{2,1,0:T(1,128)} %all-to-all-done, f32[]{:T(128)} %broadcast.2681), dimensions={1}, to_apply=%all_to_all.13.reduce_sub_computation | reduce | bytes 4194308 | tf_op jit(solution)/shard_map/all_to_all | solution.py:173
  93.8 184.2 %while.16 = (s32[]{:T(128)}, f32[8,128,64]{1,2,0:T(8,128)S(1)}, f32[8,128,64]{1,2,0:T(8,128)S(1)}, f32[8,8,8,8,64]{2,3,4,1,0:T(8,128)}, s32[8]{0:T(128)S(1)}, /*...) while((s32[]{:T(128)}, f32[8,128,64]{1,2,0:T(8,128)S(1)}, ...), condition=%wide.region_5.6_spmd.clone.clone, body=%wide.region_2.5_spmd.clone.clone.sunk | while | flops 53850804 | bytes 15474387 | solution.py:141
  95.3 18.6 %conditional.4 = (f32[8,128,64]{1,2,0:T(8,128)S(1)}, f32[8,128,64]{1,2,0:T(8,128)S(1)}, f32[1,8,8,8,64]{2,3,4,1,0:T(8,128)}) conditional(s32[]{:T(128)} %convert_element_type.412, (f32[8,128,64]{1,2,0:T(8,128)S(1)}, f32[8,128,64]{1,2,0:T(8,128)S(1)}) %tuple.139, (s32[]{:T(128)}, s32[8]{0:T(128)S(1)}, s32[8,1,1]{0,2,1:T(1,128)S(1)}, ...), branch_computations={%region_3.3_spmd, %region_4.4_spmd.clone} | conditional | flops 53850800 | bytes 11276004 | solution.py:136
  100.7 6.3 %stack.51 = f32[8,8,128,64]{2,0,3,1:T(8,128)} concatenate(f32[1,8,128,64]{2,0,3,1:T(1,128)} %bitcast.229, f32[1,8,128,64]{2,0,3,1:T(1,128)} %bitcast.228, f32[1,8,128,64]{2,0,3,1:T(1,128)} %bitcast.227, f32[1,8,128,64]{2,0,3,1:T(1,128)S(1)} %bitcast.226, f32[1,8,128,64]{2,0,3,1:T(1,128)S(1)} %bitcast.225, f32[1,8,128,64]{2,0,3,1:T(1,128)S(1)} %bitcast.224, ...), dimensions={0} | concatenate | bytes 4194304 | tf_op jit(solution)/shard_map/while/body/eval_jaxpr/cond/branch_1_fun/stack | solution.py:126
  107.0 6.9 %convolution_bitcast_fusion = f32[1,8,8,8,64]{2,3,4,1,0:T(8,128)} fusion(f32[8,8,128,64]{2,0,3,1:T(8,128)} %stack.51, f32[128,8,8,64]{0,2,3,1:T(8,128)} %get-tuple-element.428), kind=kOutput, calls=%fused_computation.4 | convolution fusion | flops 50331648 | bytes 4325376 | tf_op jit(solution)/shard_map/while/body/eval_jaxpr/cond/branch_1_fun/jgkq,kgcq->gcjq/dot_general | solution.py:127
  118.3 18.6 %conditional.4 = (f32[8,128,64]{1,2,0:T(8,128)S(1)}, f32[8,128,64]{1,2,0:T(8,128)S(1)}, f32[1,8,8,8,64]{2,3,4,1,0:T(8,128)}) conditional(s32[]{:T(128)} %convert_element_type.412, (f32[8,128,64]{1,2,0:T(8,128)S(1)}, f32[8,128,64]{1,2,0:T(8,128)S(1)}) %tuple.139, (s32[]{:T(128)}, s32[8]{0:T(128)S(1)}, s32[8,1,1]{0,2,1:T(1,128)S(1)}, ...), branch_computations={%region_3.3_spmd, %region_4.4_spmd.clone} | conditional | flops 53850800 | bytes 11276004 | solution.py:136
  130.0 6.9 %convolution_bitcast_fusion = f32[1,8,8,8,64]{2,3,4,1,0:T(8,128)} fusion(f32[8,8,128,64]{2,0,3,1:T(8,128)} %stack.51, f32[128,8,8,64]{0,2,3,1:T(8,128)} %get-tuple-element.428), kind=kOutput, calls=%fused_computation.4 | convolution fusion | flops 50331648 | bytes 4325376 | tf_op jit(solution)/shard_map/while/body/eval_jaxpr/cond/branch_1_fun/jgkq,kgcq->gcjq/dot_general | solution.py:127
  141.2 18.6 %conditional.4 = (f32[8,128,64]{1,2,0:T(8,128)S(1)}, f32[8,128,64]{1,2,0:T(8,128)S(1)}, f32[1,8,8,8,64]{2,3,4,1,0:T(8,128)}) conditional(s32[]{:T(128)} %convert_element_type.412, (f32[8,128,64]{1,2,0:T(8,128)S(1)}, f32[8,128,64]{1,2,0:T(8,128)S(1)}) %tuple.139, (s32[]{:T(128)}, s32[8]{0:T(128)S(1)}, s32[8,1,1]{0,2,1:T(1,128)S(1)}, ...), branch_computations={%region_3.3_spmd, %region_4.4_spmd.clone} | conditional | flops 53850800 | bytes 11276004 | solution.py:136
  152.9 6.9 %convolution_bitcast_fusion = f32[1,8,8,8,64]{2,3,4,1,0:T(8,128)} fusion(f32[8,8,128,64]{2,0,3,1:T(8,128)} %stack.51, f32[128,8,8,64]{0,2,3,1:T(8,128)} %get-tuple-element.428), kind=kOutput, calls=%fused_computation.4 | convolution fusion | flops 50331648 | bytes 4325376 | tf_op jit(solution)/shard_map/while/body/eval_jaxpr/cond/branch_1_fun/jgkq,kgcq->gcjq/dot_general | solution.py:127
  164.2 18.7 %conditional.4 = (f32[8,128,64]{1,2,0:T(8,128)S(1)}, f32[8,128,64]{1,2,0:T(8,128)S(1)}, f32[1,8,8,8,64]{2,3,4,1,0:T(8,128)}) conditional(s32[]{:T(128)} %convert_element_type.412, (f32[8,128,64]{1,2,0:T(8,128)S(1)}, f32[8,128,64]{1,2,0:T(8,128)S(1)}) %tuple.139, (s32[]{:T(128)}, s32[8]{0:T(128)S(1)}, s32[8,1,1]{0,2,1:T(1,128)S(1)}, ...), branch_computations={%region_3.3_spmd, %region_4.4_spmd.clone} | conditional | flops 53850800 | bytes 11276004 | solution.py:136
  175.9 6.9 %convolution_bitcast_fusion = f32[1,8,8,8,64]{2,3,4,1,0:T(8,128)} fusion(f32[8,8,128,64]{2,0,3,1:T(8,128)} %stack.51, f32[128,8,8,64]{0,2,3,1:T(8,128)} %get-tuple-element.428), kind=kOutput, calls=%fused_computation.4 | convolution fusion | flops 50331648 | bytes 4325376 | tf_op jit(solution)/shard_map/while/body/eval_jaxpr/cond/branch_1_fun/jgkq,kgcq->gcjq/dot_general | solution.py:127
  187.2 18.6 %conditional.4 = (f32[8,128,64]{1,2,0:T(8,128)S(1)}, f32[8,128,64]{1,2,0:T(8,128)S(1)}, f32[1,8,8,8,64]{2,3,4,1,0:T(8,128)}) conditional(s32[]{:T(128)} %convert_element_type.412, (f32[8,128,64]{1,2,0:T(8,128)S(1)}, f32[8,128,64]{1,2,0:T(8,128)S(1)}) %tuple.139, (s32[]{:T(128)}, s32[8]{0:T(128)S(1)}, s32[8,1,1]{0,2,1:T(1,128)S(1)}, ...), branch_computations={%region_3.3_spmd, %region_4.4_spmd.clone} | conditional | flops 53850800 | bytes 11276004 | solution.py:136
  199.0 6.9 %convolution_bitcast_fusion = f32[1,8,8,8,64]{2,3,4,1,0:T(8,128)} fusion(f32[8,8,128,64]{2,0,3,1:T(8,128)} %stack.51, f32[128,8,8,64]{0,2,3,1:T(8,128)} %get-tuple-element.428), kind=kOutput, calls=%fused_computation.4 | convolution fusion | flops 50331648 | bytes 4325376 | tf_op jit(solution)/shard_map/while/body/eval_jaxpr/cond/branch_1_fun/jgkq,kgcq->gcjq/dot_general | solution.py:127
  210.3 18.7 %conditional.4 = (f32[8,128,64]{1,2,0:T(8,128)S(1)}, f32[8,128,64]{1,2,0:T(8,128)S(1)}, f32[1,8,8,8,64]{2,3,4,1,0:T(8,128)}) conditional(s32[]{:T(128)} %convert_element_type.412, (f32[8,128,64]{1,2,0:T(8,128)S(1)}, f32[8,128,64]{1,2,0:T(8,128)S(1)}) %tuple.139, (s32[]{:T(128)}, s32[8]{0:T(128)S(1)}, s32[8,1,1]{0,2,1:T(1,128)S(1)}, ...), branch_computations={%region_3.3_spmd, %region_4.4_spmd.clone} | conditional | flops 53850800 | bytes 11276004 | solution.py:136
  222.0 6.9 %convolution_bitcast_fusion = f32[1,8,8,8,64]{2,3,4,1,0:T(8,128)} fusion(f32[8,8,128,64]{2,0,3,1:T(8,128)} %stack.51, f32[128,8,8,64]{0,2,3,1:T(8,128)} %get-tuple-element.428), kind=kOutput, calls=%fused_computation.4 | convolution fusion | flops 50331648 | bytes 4325376 | tf_op jit(solution)/shard_map/while/body/eval_jaxpr/cond/branch_1_fun/jgkq,kgcq->gcjq/dot_general | solution.py:127
  233.3 18.6 %conditional.4 = (f32[8,128,64]{1,2,0:T(8,128)S(1)}, f32[8,128,64]{1,2,0:T(8,128)S(1)}, f32[1,8,8,8,64]{2,3,4,1,0:T(8,128)}) conditional(s32[]{:T(128)} %convert_element_type.412, (f32[8,128,64]{1,2,0:T(8,128)S(1)}, f32[8,128,64]{1,2,0:T(8,128)S(1)}) %tuple.139, (s32[]{:T(128)}, s32[8]{0:T(128)S(1)}, s32[8,1,1]{0,2,1:T(1,128)S(1)}, ...), branch_computations={%region_3.3_spmd, %region_4.4_spmd.clone} | conditional | flops 53850800 | bytes 11276004 | solution.py:136
  245.0 6.9 %convolution_bitcast_fusion = f32[1,8,8,8,64]{2,3,4,1,0:T(8,128)} fusion(f32[8,8,128,64]{2,0,3,1:T(8,128)} %stack.51, f32[128,8,8,64]{0,2,3,1:T(8,128)} %get-tuple-element.428), kind=kOutput, calls=%fused_computation.4 | convolution fusion | flops 50331648 | bytes 4325376 | tf_op jit(solution)/shard_map/while/body/eval_jaxpr/cond/branch_1_fun/jgkq,kgcq->gcjq/dot_general | solution.py:127
  256.3 18.7 %conditional.4 = (f32[8,128,64]{1,2,0:T(8,128)S(1)}, f32[8,128,64]{1,2,0:T(8,128)S(1)}, f32[1,8,8,8,64]{2,3,4,1,0:T(8,128)}) conditional(s32[]{:T(128)} %convert_element_type.412, (f32[8,128,64]{1,2,0:T(8,128)S(1)}, f32[8,128,64]{1,2,0:T(8,128)S(1)}) %tuple.139, (s32[]{:T(128)}, s32[8]{0:T(128)S(1)}, s32[8,1,1]{0,2,1:T(1,128)S(1)}, ...), branch_computations={%region_3.3_spmd, %region_4.4_spmd.clone} | conditional | flops 53850800 | bytes 11276004 | solution.py:136
  268.0 6.9 %convolution_bitcast_fusion = f32[1,8,8,8,64]{2,3,4,1,0:T(8,128)} fusion(f32[8,8,128,64]{2,0,3,1:T(8,128)} %stack.51, f32[128,8,8,64]{0,2,3,1:T(8,128)} %get-tuple-element.428), kind=kOutput, calls=%fused_computation.4 | convolution fusion | flops 50331648 | bytes 4325376 | tf_op jit(solution)/shard_map/while/body/eval_jaxpr/cond/branch_1_fun/jgkq,kgcq->gcjq/dot_general | solution.py:127
  278.0 8.5 %multiply_reduce_fusion = f32[8,8,8]{0,2,1:T(8,128)S(1)} fusion(f32[64]{0:T(128)S(1)} %compare_select_fusion.9, f32[8,8]{1,0:T(8,128)S(1)} %sqrt_multiply_fusion, f32[8,8,8,8,64]{2,3,4,1,0:T(8,128)} %get-tuple-element.216), kind=kLoop, calls=%fused_computation.97 | loop fusion | flops 1048064 | bytes 1051136 | tf_op jit(solution)/shard_map/reduce_sum | solution.py:152
  294.0 11.1 %copy.62 = f32[8,8,8,8,64]{4,3,2,1,0:T(8,128)} copy(f32[8,8,8,8,64]{1,3,4,0,2:T(8,128)} %bitcast.221) | data formatting | bytes 2097152 | tf_op jit(solution)/shard_map/transpose | solution.py:144
  305.1 6.3 %collective-permute-start.3 = (f32[4,64]{1,0:T(4,128)S(1)}, f32[4,64]{1,0:T(4,128)S(1)}, u32[]{:S(2)}, u32[]{:S(2)}) collective-permute-start(f32[4,64]{1,0:T(4,128)S(1)} %add.499), channel_id=1, source_target_pairs={{0,16},{2,18},{4,20},{6,22},{8,24},{10,26},{12,28},{14,30},{16,0},... | collective-permute-start | bytes 3080 | tf_op jit(solution)/shard_map/ppermute | solution.py:182
  (313 shorter events, 155.4 us)
Async XLA Ops:
  0.6 1.6 copy-start
  18.8 51.5 %all-to-all-start = ((f32[16,1,32768]{2,1,0:T(1,128)}), f32[16,1,32768]{2,1,0:T(1,128)}, u32[]{:S(2)}, u32[]{:S(2)}) async-start(f32[16,1,32768]{2,1,0:T(1,128)} %reshape.2457), calls=%async_computation | async-start | bytes 4194304 | tf_op jit(solution)/shard_map/all_to_all | solution.py:173
  94.0 1.3 copy-start.1
  113.9 3.1 copy-start.2
  117.0 1.2 copy-start.1
  136.9 3.1 copy-start.2
  140.0 1.2 copy-start.1
  159.9 3.1 copy-start.2
  163.0 1.2 copy-start.1
  182.9 3.1 copy-start.2
  186.0 1.2 copy-start.1
  205.9 3.1 copy-start.2
  209.0 1.2 copy-start.1
  228.9 3.1 copy-start.2
  232.0 1.2 copy-start.1
  251.9 3.1 copy-start.2
  255.0 1.2 copy-start.1
  274.9 3.1 copy-start.2
  286.7 3.7 %collective-permute-start = (f32[4,64]{1,0:T(4,128)S(1)}, f32[4,64]{1,0:T(4,128)S(1)}, u32[]{:S(2)}, u32[]{:S(2)}) collective-permute-start(f32[4,64]{1,0:T(4,128)S(1)} %broadcast_divide_fusion), channel_id=1, source_target_pairs={{0,2},{2,0},{4,6},{6,4},{8,10},{10,8},{12,14},{14,12},{16,18},{18,... | collective-permute-start | bytes 3080 | tf_op jit(solution)/shard_map/ppermute | solution.py:182
  290.4 3.6 %collective-permute-start.1 = (f32[4,64]{1,0:T(4,128)S(1)}, f32[4,64]{1,0:T(4,128)S(1)}, u32[]{:S(2)}, u32[]{:S(2)}) collective-permute-start(f32[4,64]{1,0:T(4,128)S(1)} %fusion.102), channel_id=1, source_target_pairs={{0,4},{2,6},{4,0},{6,2},{8,12},{10,14},{12,8},{14,10},{16,20},{18,... | collective-permute-start | bytes 3080 | tf_op jit(solution)/shard_map/ppermute | solution.py:182
  294.0 11.1 %collective-permute-start.2 = (f32[4,64]{1,0:T(4,128)S(1)}, f32[4,64]{1,0:T(4,128)S(1)}, u32[]{:S(2)}, u32[]{:S(2)}) collective-permute-start(f32[4,64]{1,0:T(4,128)S(1)} %add.498), channel_id=1, source_target_pairs={{0,8},{2,10},{4,12},{6,14},{8,0},{10,2},{12,4},{14,6},{16,24},{18,... | collective-permute-start | bytes 3080 | tf_op jit(solution)/shard_map/ppermute | solution.py:182
  305.1 9.6 %collective-permute-start.3 = (f32[4,64]{1,0:T(4,128)S(1)}, f32[4,64]{1,0:T(4,128)S(1)}, u32[]{:S(2)}, u32[]{:S(2)}) collective-permute-start(f32[4,64]{1,0:T(4,128)S(1)} %add.499), channel_id=1, source_target_pairs={{0,16},{2,18},{4,20},{6,22},{8,24},{10,26},{12,28},{14,30},{16,0},... | collective-permute-start | bytes 3080 | tf_op jit(solution)/shard_map/ppermute | solution.py:182
